TPU v7x, 32 devices: a whole 2x2x4 slice. The times are simulated.
32 devices in a mesh: own: 8 (over z, y), blk: 4 (over x, core).
Axes of the slice: x: 2, y: 2, z: 4, core: 2. Of those that a mesh axis runs over, the one named last changes fastest.
Arguments:
- points: bfloat16 [64, 4096], P(None, ('own', 'blk')), may hold values from -6 to 6
- solution_field: float32 [33, 4096], P(None, ('own', 'blk')), may hold values from -6 to 6
- residual: float32 [33, 4096], P(None, ('own', 'blk')), may hold values from -12 to 12
- direction: float32 [33, 4096], P(None, ('own', 'blk')), may hold values from -12 to 12
Outputs:
- solution_next: float32 [33, 4096], P(None, ('own', 'blk'))
- residual_next: float32 [33, 4096], P(None, ('own', 'blk'))
- direction_next: float32 [33, 4096], P(None, ('own', 'blk'))
All inputs are finite; a program needn't handle non-finite values.
Results may differ from a plain program's by a relative error of at most 0.0027.
Values may be sent and summed in bfloat16 or wider, within the bound.
A program may use at most 64 MiB of HBM per device.

v0:
```python
import math

import jax
import jax.numpy as jnp
from jax import lax
from jax.sharding import PartitionSpec as P

amplitude = 1.0
decay_rate = 1.0 / 16.0
noise_level = 0.5


def tile_products(row_blocks, row_norms, columns, dirs):
    col_norms = jnp.sum(jnp.square(columns.astype(jnp.float32)), axis=0)

    def single(pair):
        rows, norms = pair
        inner = lax.dot_general(
            rows, columns, (((0,), (0,)), ((), ())), preferred_element_type=jnp.float32
        )
        dist = jnp.maximum(norms[:, None] + col_norms[None, :] - 2.0 * inner, 0.0)
        kern = (amplitude * jnp.exp(-decay_rate * dist)).astype(jnp.bfloat16)
        return lax.dot_general(
            dirs, kern, (((1,), (1,)), ((), ())), preferred_element_type=jnp.float32
        )

    return lax.map(single, (row_blocks, row_norms))


def split_rows(rows):
    width = rows.shape[1]
    size = math.gcd(width, 512)
    count = width // size
    blocks = rows.reshape(rows.shape[0], count, size).transpose(1, 0, 2)
    norms = jnp.sum(jnp.square(blocks.astype(jnp.float32)), axis=1)
    return (blocks, norms)


def local(points, solution_field, residual, direction):
    dir_low = direction.astype(jnp.bfloat16)
    count_rhs = direction.shape[0]
    rows = lax.all_gather(points, "own", axis=1, tiled=True)
    blocks, norms = split_rows(rows)
    total = tile_products(
        blocks,
        norms,
        lax.all_gather(points, "blk", axis=1, tiled=True),
        lax.all_gather(dir_low, "blk", axis=1, tiled=True),
    )
    partial_value = total.transpose(1, 0, 2).reshape(count_rhs, rows.shape[1])
    mine = lax.psum_scatter(partial_value, "own", scatter_dimension=1, tiled=True)
    image = mine + noise_level * direction
    rr_sum, pq_sum, rq_sum, qq_sum = lax.psum(
        (
            jnp.sum(residual * residual, axis=1),
            jnp.sum(direction * image, axis=1),
            jnp.sum(residual * image, axis=1),
            jnp.sum(image * image, axis=1),
        ),
        ("own", "blk"),
    )
    alpha = rr_sum / pq_sum
    residual_next = residual - alpha[:, None] * image
    new_sum = rr_sum - 2.0 * alpha * rq_sum + alpha * alpha * qq_sum
    solution_next = solution_field + alpha[:, None] * direction
    direction_next = residual_next + (new_sum / rr_sum)[:, None] * direction
    return (solution_next, residual_next, direction_next)


def solution(mesh):
    in_specs = (
        P(None, ("own", "blk")),
        P(None, ("own", "blk")),
        P(None, ("own", "blk")),
        P(None, ("own", "blk")),
    )
    out_specs = (P(None, ("own", "blk")), P(None, ("own", "blk")), P(None, ("own", "blk")))
    return jax.shard_map(local, mesh=mesh, in_specs=in_specs, out_specs=out_specs, check_vma=False)
```

profile of v0, /device:TPU:0, one launch (start us, length us, event | category | flops | bytes accessed | tf_op | source)
XLA Modules:
  0.0 152.2 jit_solution(9612652688748072945)
XLA Ops:
  7.2 0.0 copy-start.3
  7.2 0.0 reduce-scatter.2.cloned.1.call-start
  7.2 28.2 %all_gather.9 = bf16[64,1024]{1,0:T(8,128)(2,1)S(1)} all-gather(bf16[64,128]{1,0:T(8,128)(2,1)} %param.6), channel_id=1, replica_groups=mesh['own'=8,'blk'=4] {'own'}, dimensions={1}, use_global_device_ids=true | all-gather | bytes 147456 | tf_op jit(solution)/shard_map/all_gather | solution.py:42
  35.4 0.0 copy-done.3
  35.4 5.3 %all_gather.10 = bf16[64,512]{1,0:T(8,128)(2,1)S(1)} all-gather(bf16[64,128]{1,0:T(8,128)(2,1)S(1)} %copy-done.3), channel_id=1, replica_groups=mesh['own'=8,'blk'=4] {'blk'}, dimensions={1}, use_global_device_ids=true | all-gather | bytes 81920 | tf_op jit(solution)/shard_map/all_gather | solution.py:47
  40.6 0.1 reshape.17
  40.7 0.2 multiply_reduce_fusion
  40.9 0.0 copy-start
  40.9 0.7 copy-done
  41.6 5.2 %all_gather.11 = bf16[33,512]{1,0:T(8,128)(2,1)S(1)} all-gather(bf16[33,128]{1,0:T(8,128)(2,1)S(1)} %convert_element_type.14), channel_id=1, replica_groups=mesh['own'=8,'blk'=4] {'blk'}, dimensions={1}, use_global_device_ids=true | all-gather | bytes 42240 | tf_op jit(solution)/shard_map/all_gather | solution.py:48
  46.8 1.2 while.10
  46.8 0.6 fusion.32
  47.5 0.6 fusion.32
  48.0 0.1 copy.9
  48.2 0.1 pad
  48.2 0.7 copy.10
  48.9 0.0 copy-start.1
  48.9 0.0 reduce-scatter.2.cloned.1.call-update
  49.0 54.6 %reduce-scatter.2.cloned.1.call-done = f32[33,128]{1,0:T(8,128)} async-done(((f32[33,1024]{1,0:T(8,128)}), f32[33,128]{1,0:T(8,128)}) %reduce-scatter.2.cloned.1.call-update) | async-done | bytes 16912 | tf_op jit(solution)/shard_map/reduce_scatter | solution.py:51
  103.6 0.0 copy-done.1
  103.6 0.0 copy-start.4
  103.6 0.9 multiply_reduce_fusion.3
  104.4 0.0 copy-start.2
  104.5 40.2 %all-reduce = (f32[33]{0:T(128)S(1)}, f32[33]{0:T(128)S(1)}, f32[33]{0:T(128)S(1)}, f32[33]{0:T(128)S(1)}) all-reduce(f32[33]{0:T(128)S(1)} %get-tuple-element.51, f32[33]{0:T(128)S(1)} %get-tuple-element.50, f32[33]{0:T(128)S(1)} %get-tuple-element.49, f32[33]{0:T(128)S(1)} %get-tuple-element.48), channel_id=1, replica_groups=mesh['own'=8,'blk'=4] {'own','blk'}, use_global_device_ids=true, to_apply=%region_1.0 | all-reduce | flops 132 | bytes 1056 | tf_op jit(solution)/shard_map/psum | solution.py:53
  144.6 0.0 copy-done.4
  144.6 0.0 copy-done.2
  144.7 0.7 multiply_add_fusion
  (7 shorter events, 0.1 us)
Async XLA Ops:
  7.2 28.2 %copy-start.3 = (bf16[64,128]{1,0:T(8,128)(2,1)S(1)}, bf16[64,128]{1,0:T(8,128)(2,1)}, u32[]{:S(2)}) copy-start(bf16[64,128]{1,0:T(8,128)(2,1)} %param.6) | copy-start | bytes 49156
  7.2 96.4 %reduce-scatter.2.cloned.1.call-start = ((), (), s32[]{:S(2)}) async-start(), calls=%async_computation.1 | async-start | bytes 184320 | tf_op jit(solution)/shard_map/reduce_scatter | solution.py:51
  40.9 0.7 copy-start
  48.9 54.6 %copy-start.1 = (f32[33,128]{1,0:T(8,128)S(1)}, f32[33,128]{1,0:T(8,128)}, u32[]{:S(2)}) copy-start(f32[33,128]{1,0:T(8,128)} %param.8) | copy-start | bytes 50692
  103.6 41.1 %copy-start.4 = (f32[33,128]{1,0:T(8,128)S(1)}, f32[33,128]{1,0:T(8,128)}, u32[]{:S(2)}) copy-start(f32[33,128]{1,0:T(8,128)} %param.7) | copy-start | bytes 50692
  104.4 40.2 %copy-start.2 = (f32[33,128]{1,0:T(8,128)S(1)}, f32[33,128]{1,0:T(8,128)}, u32[]{:S(2)}) copy-start(f32[33,128]{1,0:T(8,128)} %reduce-scatter.2.cloned.1.call-done) | copy-start | bytes 50692
Sparse Core Ops, SparseCore 0:
  49.1 54.4 reduce-scatter.1
where the time goes:
time: 153 us; the launch traced here: 152 us
  blocking collectives  78.8 us (52%)
  waiting for transfers between devices  54.6 us (36%)
  between operations  14.1 us (9%)
  other arithmetic  1.81 us (1%)
  local copies, waits for them, and re-layouts  1.69 us (1%)
    reduce_scatter x1, waiting for transfers between devices, local(): lax.psum_scatter(partial_value, 'own', scatter_dimension=1, tiled=True)  54.6 us
    psum x1, blocking collectives, local(): lax.psum((jnp.sum(residual * residual, axis=1), jnp.sum(direction * image...  40.2 us
    all_gather x1, blocking collectives, local(): rows = lax.all_gather(points, 'own', axis=1, tiled=True)  28.2 us
    all_gather x1, blocking collectives, local(): lax.all_gather(points, 'blk', axis=1, tiled=True)  5.25 us
    all_gather x1, blocking collectives, local(): lax.all_gather(dir_low, 'blk', axis=1, tiled=True)  5.18 us
  transfers between devices with their start and end apart: 1, of which 1 were waited for; matrix products, arithmetic and copies ran while one was open for 0% of the time, Pallas kernels for 0%

commit v1 on v0

v1 whole, which is shorter than its diff:
```python
import functools
import math

import jax
import jax.numpy as jnp
from jax import lax
from jax.experimental import pallas as pl
from jax.experimental.pallas import tpu as pltpu
from jax.sharding import PartitionSpec as P

amplitude = 1.0
decay_rate = 1.0 / 16.0
noise_level = 0.5

LOG2E = math.log2(math.e)
MESH = pl.DeviceIdType.MESH


def split_own(n_own, n_blk):
    for low in range(1, n_own + 1):
        if n_own % low == 0 and low * n_blk > n_own // low:
            return low
    return n_own


def wait_bytes(ref, sem):
    pltpu.make_async_copy(ref, ref, sem).wait()


def kernel(n_own, n_blk, low, points_ref, solution_ref, residual_ref, direction_ref,
           solution_out, residual_out, direction_out,
           rows_ref, cols_ref, norms_ref, acc_ref, part_ref, back_ref, sums_ref,
           row_send, row_recv, col_send, col_recv, part_send, part_recv, sum_send, sum_recv):
    high = n_own // low
    n_row, n_col = low * n_blk, high
    dim, width = points_ref.shape
    rhs = direction_ref.shape[0]
    own, blk = lax.axis_index("own"), lax.axis_index("blk")
    h, l = own // low, own % low
    r = l * n_blk + blk
    scale = decay_rate * LOG2E

    def row_peer(k):
        other = (r + k) % n_row
        return (h * low + other // n_blk, other % n_blk)

    def col_peer(k):
        return (((h + k) % high) * low + l, blk)

    barrier = pltpu.get_barrier_semaphore()
    for k in range(1, n_col):
        pl.semaphore_signal(barrier, inc=1, device_id=col_peer(k), device_id_type=MESH)
    for k in range(1, n_row):
        pl.semaphore_signal(barrier, inc=1, device_id=row_peer(k), device_id_type=MESH)

    cols_ref[0, :dim, :] = points_ref[...]
    cols_ref[0, dim:, :] = jnp.zeros(cols_ref.shape[1:], jnp.bfloat16)[dim:]
    cols_ref[0, dim:dim + rhs, :] = direction_ref[...].astype(jnp.bfloat16)
    rows_ref[:, :width] = points_ref[...]

    pl.semaphore_wait(barrier, n_row + n_col - 2)

    col_copies = []
    for k in range(1, n_col):
        slot = n_col - k
        copy = pltpu.make_async_remote_copy(
            src_ref=cols_ref.at[0], dst_ref=cols_ref.at[slot], send_sem=col_send.at[slot],
            recv_sem=col_recv.at[slot], device_id=col_peer(k), device_id_type=MESH)
        copy.start()
        col_copies.append(copy)
    row_copies = []
    for k in range(1, n_row):
        slot = n_row - k
        copy = pltpu.make_async_remote_copy(
            src_ref=points_ref, dst_ref=rows_ref.at[:, pl.ds(slot * width, width)],
            send_sem=row_send.at[slot], recv_sem=row_recv.at[slot],
            device_id=row_peer(k), device_id_type=MESH)
        copy.start()
        row_copies.append(copy)

    diag = (lax.broadcasted_iota(jnp.int32, (rhs, width), 0)
            == lax.broadcasted_iota(jnp.int32, (rhs, width), 1))

    def to_row(products):
        column = jnp.sum(products, axis=1, keepdims=True)
        return jnp.sum(jnp.where(diag, column, 0.0), axis=0, keepdims=True)

    def to_column(row):
        return jnp.sum(jnp.where(diag, row, 0.0), axis=1, keepdims=True)

    residual = residual_ref[...]
    direction = direction_ref[...]
    sums_ref[0, 0:1, :] = to_row(residual * residual)

    for copy in row_copies:
        copy.wait_recv()
    chunk = math.gcd(n_row * width, 2 * width)
    n_chunk = n_row * width // chunk
    for c in range(n_chunk):
        wide = rows_ref[:, c * chunk:(c + 1) * chunk].astype(jnp.float32)
        norms_ref[:, c * chunk:(c + 1) * chunk] = jnp.sum(wide * wide, axis=0, keepdims=True) * scale

    part_copies = []
    per = chunk // width
    for k in range(n_col):
        if k > 0:
            wait_bytes(cols_ref.at[k], col_recv.at[k])
        wide = cols_ref[k, :dim, :].astype(jnp.float32).T
        col_norms = jnp.sum(wide * wide, axis=1, keepdims=True) * scale
        turned = wide.astype(jnp.bfloat16)
        dirs = cols_ref[k, dim:, :]
        for c in range(n_chunk):
            at = slice(c * chunk, (c + 1) * chunk)
            inner = jnp.dot(turned, rows_ref[:, at], preferred_element_type=jnp.float32)
            power = jnp.minimum(inner * (2.0 * scale) - norms_ref[:, at] - col_norms, 0.0)
            kern = (amplitude * jnp.exp2(power)).astype(jnp.bfloat16)
            value = jnp.dot(dirs, kern, preferred_element_type=jnp.float32)
            if k > 0:
                value += acc_ref[:, at]
            if k < n_col - 1:
                acc_ref[:, at] = value
                continue
            for j in range(per):
                to = c * per + j
                piece = value[:, j * width:(j + 1) * width]
                if to == 0:
                    acc_ref[:, :width] = piece
                    continue
                part_ref[to] = piece.astype(jnp.bfloat16)
                slot = n_row - to
                copy = pltpu.make_async_remote_copy(
                    src_ref=part_ref.at[to], dst_ref=back_ref.at[slot],
                    send_sem=part_send.at[slot], recv_sem=part_recv.at[slot],
                    device_id=row_peer(to), device_id_type=MESH)
                copy.start()
                part_copies.append(copy)

    image = acc_ref[:, :width]
    for k in range(1, n_row):
        wait_bytes(back_ref.at[k], part_recv.at[k])
        image += back_ref[k].astype(jnp.float32)
    image = image[:rhs] + noise_level * direction

    sums_ref[0, 1:2, :] = to_row(direction * image)
    sums_ref[0, 2:3, :] = to_row(residual * image)
    sums_ref[0, 3:4, :] = to_row(image * image)
    n_all = n_own * n_blk

    def send_sums(k, carry):
        peer = ((own + k // n_blk) % n_own, (blk + k % n_blk) % n_blk)
        slot = ((n_own - k // n_blk) % n_own) * n_blk + (n_blk - k % n_blk) % n_blk
        pltpu.make_async_remote_copy(
            src_ref=sums_ref.at[0], dst_ref=sums_ref.at[slot], send_sem=sum_send,
            recv_sem=sum_recv, device_id=peer, device_id_type=MESH).start()
        return carry

    lax.fori_loop(1, n_all, send_sums, 0)

    for copy in col_copies + row_copies + part_copies:
        copy.wait_send()
    wait_bytes(sums_ref.at[pl.ds(1, n_all - 1)], sum_send)
    wait_bytes(sums_ref.at[pl.ds(1, n_all - 1)], sum_recv)
    total = jnp.sum(sums_ref[...], axis=0)
    rr, pq, rq, qq = (total[i:i + 1] for i in range(4))
    alpha_row = rr / pq
    new_sum = rr - 2.0 * alpha_row * rq + alpha_row * alpha_row * qq
    alpha = to_column(alpha_row)
    beta = to_column(new_sum / rr)
    residual_next = residual - alpha * image
    residual_out[...] = residual_next
    solution_out[...] = solution_ref[...] + alpha * direction
    direction_out[...] = residual_next + beta * direction


def local(n_own, n_blk, points, solution_field, residual, direction):
    low = split_own(n_own, n_blk)
    n_row, n_col = low * n_blk, n_own // low
    dim, width = points.shape
    rhs = direction.shape[0]
    padded = -(-rhs // 16) * 16
    vmem = pl.BlockSpec(memory_space=pltpu.VMEM)
    out = jax.ShapeDtypeStruct(direction.shape, jnp.float32)
    dma = pltpu.SemaphoreType.DMA
    return pl.pallas_call(
        functools.partial(kernel, n_own, n_blk, low),
        out_shape=(out, out, out),
        in_specs=[vmem] * 4,
        out_specs=(vmem,) * 3,
        scratch_shapes=[
            pltpu.VMEM((dim, n_row * width), jnp.bfloat16),
            pltpu.VMEM((n_col, dim + padded, width), jnp.bfloat16),
            pltpu.VMEM((1, n_row * width), jnp.float32),
            pltpu.VMEM((padded, n_row * width), jnp.float32),
            pltpu.VMEM((n_row, padded, width), jnp.bfloat16),
            pltpu.VMEM((n_row, padded, width), jnp.bfloat16),
            pltpu.VMEM((n_own * n_blk, 4, width), jnp.float32),
            dma((n_row,)), dma((n_row,)), dma((n_col,)), dma((n_col,)),
            dma((n_row,)), dma((n_row,)), dma, dma,
        ],
        compiler_params=pltpu.CompilerParams(collective_id=0, has_side_effects=True),
    )(points, solution_field, residual, direction)


def solution(mesh):
    spec = P(None, ("own", "blk"))
    body = functools.partial(local, mesh.shape["own"], mesh.shape["blk"])
    return jax.shard_map(body, mesh=mesh, in_specs=(spec,) * 4, out_specs=(spec,) * 3, check_vma=False)
```

time: 153 us -> 25.7 us (0.17)
  blocking collectives: 78.8 us -> 0 us
  waiting for transfers between devices: 54.6 us -> 0 us
  Pallas kernels: 0 us -> 22.1 us
  between operations: 14.1 us -> 0.65 us
  other arithmetic: 1.81 us -> 0 us
    reduce_scatter x1 -> x0, waiting for transfers between devices: 54.6 us -> none  [local(): lax.psum_scatter(partial_value, 'own', scatter_dimension=1, tiled=True)]
    psum x1 -> x0, blocking collectives: 40.2 us -> none  [local(): lax.psum((jnp.sum(residual * residual, axis=1), jnp.sum(direction * image...]
    all_gather x3 -> x0, blocking collectives: 38.6 us -> none  [the longest x1 28.2 us: local(): rows = lax.all_gather(points, 'own', axis=1, tiled=True)]
    pallas_call x0 -> x1, Pallas kernels: none -> 22.1 us  [local(): pl.pallas_call(functools.partial(kernel, n_own, n_blk, low), out_shape=(o...]
  transfers between devices with their start and end apart: 1 -> 0, of which waited for: 1 -> 0; matrix products, arithmetic and copies ran while one was open for 0% -> 0% of each run, Pallas kernels for 0% -> 0%
where the time goes in v1:
time: 25.7 us; the launch traced here: 25.4 us
  Pallas kernels  22.1 us (86%)
  local copies, waits for them, and re-layouts  2.69 us (10%)
  between operations  0.65 us (3%)
    pallas_call x1, Pallas kernels, local(): pl.pallas_call(functools.partial(kernel, n_own, n_blk, low), out_shape=(o...  22.1 us
    unnamed x7, local copies, waits for them, and re-layouts  2.69 us

profile of v1, /device:TPU:0, one launch (start us, length us, event | category | flops | bytes accessed | tf_op | source)
XLA Modules:
  0.0 25.4 jit_solution(3233032026918421780)
XLA Ops:
  0.6 22.1 %shard_map.67 = (f32[33,128]{1,0:T(8,128)}, f32[33,128]{1,0:T(8,128)}, f32[33,128]{1,0:T(8,128)}) custom-call(bf16[64,128]{1,0:T(8,128)(2,1)} %points_ref.1, f32[33,128]{1,0:T(8,128)} %solution_ref.1, f32[33,128]{1,0:T(8,128)} %residual_ref.1, f32[33,128]{1,0:T(8,128)} %direction_ref.1), custom_call_target="tpu_custom_call" | custom-call | tf_op jit(solution)/shard_map/pallas_call | solution.py:184
  22.7 0.0 copy-start.1
  22.7 1.3 %copy.10 = f32[33,128]{1,0:T(8,128)} copy(f32[33,128]{1,0:T(8,128)} %get-tuple-element.6) | data formatting | bytes 33792
  24.1 0.0 copy-done.1
  24.1 0.0 copy-start
  24.1 0.6 %copy.11 = f32[33,128]{1,0:T(8,128)} copy(f32[33,128]{1,0:T(8,128)S(1)} %copy-done.1) | data formatting | bytes 33792
  24.7 0.1 copy-done
  24.8 0.6 %copy.12 = f32[33,128]{1,0:T(8,128)} copy(f32[33,128]{1,0:T(8,128)S(1)} %copy-done) | data formatting | bytes 33792
Async XLA Ops:
  22.7 1.4 %copy-start.1 = (f32[33,128]{1,0:T(8,128)S(1)}, f32[33,128]{1,0:T(8,128)}, u32[]{:S(2)}) copy-start(f32[33,128]{1,0:T(8,128)} %get-tuple-element.7) | copy-start | bytes 50692
  24.1 0.7 %copy-start = (f32[33,128]{1,0:T(8,128)S(1)}, f32[33,128]{1,0:T(8,128)}, u32[]{:S(2)}) copy-start(f32[33,128]{1,0:T(8,128)} %get-tuple-element.8) | copy-start | bytes 50692

commit v2 on v1

--- a/solution.py
+++ b/solution.py
@@ -27,25 +27,40 @@
     pltpu.make_async_copy(ref, ref, sem).wait()
 
 
-def kernel(n_own, n_blk, low, points_ref, solution_ref, residual_ref, direction_ref,
-           solution_out, residual_out, direction_out,
-           rows_ref, cols_ref, norms_ref, acc_ref, part_ref, back_ref, sums_ref,
+def kernel(n_own, n_blk, low, points_hbm, residual_hbm, direction_hbm, image_out, alpha_out, beta_out,
+           points_ref, residual_ref, direction_ref, load_sem, rows_ref, cols_ref, norms_ref, acc_ref, part_ref, back_ref, sums_ref, square_ref,
            row_send, row_recv, col_send, col_recv, part_send, part_recv, sum_send, sum_recv):
     high = n_own // low
     n_row, n_col = low * n_blk, high
     dim, width = points_ref.shape
     rhs = direction_ref.shape[0]
+    loads = [
+        pltpu.make_async_copy(points_hbm, points_ref, load_sem.at[0]),
+        pltpu.make_async_copy(direction_hbm, direction_ref, load_sem.at[1]),
+        pltpu.make_async_copy(residual_hbm, residual_ref, load_sem.at[2]),
+    ]
+    for load in loads:
+        load.start()
     own, blk = lax.axis_index("own"), lax.axis_index("blk")
-    h, l = own // low, own % low
+    h, l = lax.div(own, low), lax.rem(own, low)
     r = l * n_blk + blk
     scale = decay_rate * LOG2E
 
     def row_peer(k):
-        other = (r + k) % n_row
-        return (h * low + other // n_blk, other % n_blk)
+        other = lax.rem(r + k, n_row)
+        return (h * low + lax.div(other, n_blk), lax.rem(other, n_blk))
+
+    paired = n_col & (n_col - 1) == 0
 
     def col_peer(k):
-        return (((h + k) % high) * low + l, blk)
+        if not paired:
+            return (lax.rem(h + k, high) * low + l, blk)
+        other, bit = h, 1
+        while bit <= k:
+            if k & bit:
+                other = other + bit - 2 * bit * lax.rem(lax.div(h, bit), 2)
+            bit *= 2
+        return (other * low + l, blk)
 
     barrier = pltpu.get_barrier_semaphore()
     for k in range(1, n_col):
@@ -53,6 +68,8 @@
     for k in range(1, n_row):
         pl.semaphore_signal(barrier, inc=1, device_id=row_peer(k), device_id_type=MESH)
 
+    for load in loads:
+        load.wait()
     cols_ref[0, :dim, :] = points_ref[...]
     cols_ref[0, dim:, :] = jnp.zeros(cols_ref.shape[1:], jnp.bfloat16)[dim:]
     cols_ref[0, dim:dim + rhs, :] = direction_ref[...].astype(jnp.bfloat16)
@@ -61,8 +78,8 @@
     pl.semaphore_wait(barrier, n_row + n_col - 2)
 
     col_copies = []
-    for k in range(1, n_col):
-        slot = n_col - k
+    for k in reversed(range(1, n_col)):
+        slot = k if paired else n_col - k
         copy = pltpu.make_async_remote_copy(
             src_ref=cols_ref.at[0], dst_ref=cols_ref.at[slot], send_sem=col_send.at[slot],
             recv_sem=col_recv.at[slot], device_id=col_peer(k), device_id_type=MESH)
@@ -78,19 +95,50 @@
         copy.start()
         row_copies.append(copy)
 
-    diag = (lax.broadcasted_iota(jnp.int32, (rhs, width), 0)
-            == lax.broadcasted_iota(jnp.int32, (rhs, width), 1))
-
-    def to_row(products):
-        column = jnp.sum(products, axis=1, keepdims=True)
-        return jnp.sum(jnp.where(diag, column, 0.0), axis=0, keepdims=True)
-
-    def to_column(row):
-        return jnp.sum(jnp.where(diag, row, 0.0), axis=1, keepdims=True)
+    row_at = lax.broadcasted_iota(jnp.int32, (rhs, width), 0)
+    lane_at = lax.broadcasted_iota(jnp.int32, (rhs, width), 1)
+    n_all = n_own * n_blk
+
+    def place(i, count):
+        packed = count * rhs <= width
+        return (0, i * rhs) if packed else (i, 0)
+
+    def to_sums(products, ref):
+        for line in range(ref.shape[1]):
+            spread = jnp.zeros((rhs, width), jnp.float32)
+            for i, product in enumerate(products):
+                at, shift = place(i, len(products))
+                if at == line:
+                    column = jnp.sum(product, axis=1, keepdims=True)
+                    spread = jnp.where(lane_at == row_at + shift, column, spread)
+            ref[0, line:line + 1, :] = jnp.sum(spread, axis=0, keepdims=True)
+
+    def unpack(ref, i, count):
+        at, shift = place(i, count)
+        row = jnp.sum(ref[:, at, :], axis=0, keepdims=True)
+        return jnp.sum(jnp.where(lane_at == row_at + shift, row, 0.0), axis=1, keepdims=True)
+
+    def exchange(ref, send_sem, recv_sem):
+        def send(k, carry):
+            up, over = k // n_blk, k % n_blk
+            peer = (lax.rem(own + up, n_own), lax.rem(blk + over, n_blk))
+            slot = lax.rem(n_own - up, n_own) * n_blk + lax.rem(n_blk - over, n_blk)
+            pltpu.make_async_remote_copy(
+                src_ref=ref.at[0], dst_ref=ref.at[slot], send_sem=send_sem,
+                recv_sem=recv_sem, device_id=peer, device_id_type=MESH).start()
+            return carry
+
+        lax.fori_loop(1, n_all, send, 0, unroll=n_all <= 64)
+
+        def finish():
+            wait_bytes(ref.at[pl.ds(1, n_all - 1)], send_sem)
+            wait_bytes(ref.at[pl.ds(1, n_all - 1)], recv_sem)
+
+        return finish
 
     residual = residual_ref[...]
     direction = direction_ref[...]
-    sums_ref[0, 0:1, :] = to_row(residual * residual)
+    to_sums([residual * residual], square_ref)
 
     for copy in row_copies:
         copy.wait_recv()
@@ -135,41 +183,33 @@
                 copy.start()
                 part_copies.append(copy)
 
+    early = exchange(square_ref, sum_send.at[1], sum_recv.at[1])
     image = acc_ref[:, :width]
     for k in range(1, n_row):
         wait_bytes(back_ref.at[k], part_recv.at[k])
         image += back_ref[k].astype(jnp.float32)
     image = image[:rhs] + noise_level * direction
 
-    sums_ref[0, 1:2, :] = to_row(direction * image)
-    sums_ref[0, 2:3, :] = to_row(residual * image)
-    sums_ref[0, 3:4, :] = to_row(image * image)
-    n_all = n_own * n_blk
-
-    def send_sums(k, carry):
-        peer = ((own + k // n_blk) % n_own, (blk + k % n_blk) % n_blk)
-        slot = ((n_own - k // n_blk) % n_own) * n_blk + (n_blk - k % n_blk) % n_blk
-        pltpu.make_async_remote_copy(
-            src_ref=sums_ref.at[0], dst_ref=sums_ref.at[slot], send_sem=sum_send,
-            recv_sem=sum_recv, device_id=peer, device_id_type=MESH).start()
-        return carry
-
-    lax.fori_loop(1, n_all, send_sums, 0)
-
+    to_sums([direction * image, residual * image, image * image], sums_ref)
+    late = exchange(sums_ref, sum_send.at[0], sum_recv.at[0])
+    image_out[...] = image
     for copy in col_copies + row_copies + part_copies:
         copy.wait_send()
-    wait_bytes(sums_ref.at[pl.ds(1, n_all - 1)], sum_send)
-    wait_bytes(sums_ref.at[pl.ds(1, n_all - 1)], sum_recv)
-    total = jnp.sum(sums_ref[...], axis=0)
-    rr, pq, rq, qq = (total[i:i + 1] for i in range(4))
-    alpha_row = rr / pq
-    new_sum = rr - 2.0 * alpha_row * rq + alpha_row * alpha_row * qq
-    alpha = to_column(alpha_row)
-    beta = to_column(new_sum / rr)
-    residual_next = residual - alpha * image
+    early()
+    late()
+    rr = unpack(square_ref, 0, 1)
+    pq, rq, qq = (unpack(sums_ref, i, 3) for i in range(3))
+    alpha = rr / pq
+    new_sum = rr - 2.0 * alpha * rq + alpha * alpha * qq
+    alpha_out[...] = jnp.broadcast_to(alpha, (rhs, width))
+    beta_out[...] = jnp.broadcast_to(new_sum / rr, (rhs, width))
+
+
+def update(image, alpha, beta, solution_field, residual, direction, solution_out, residual_out, direction_out):
+    residual_next = residual[...] - alpha[...] * image[...]
     residual_out[...] = residual_next
-    solution_out[...] = solution_ref[...] + alpha * direction
-    direction_out[...] = residual_next + beta * direction
+    solution_out[...] = solution_field[...] + alpha[...] * direction[...]
+    direction_out[...] = residual_next + beta[...] * direction[...]
 
 
 def local(n_own, n_blk, points, solution_field, residual, direction):
@@ -181,24 +221,32 @@
     vmem = pl.BlockSpec(memory_space=pltpu.VMEM)
     out = jax.ShapeDtypeStruct(direction.shape, jnp.float32)
     dma = pltpu.SemaphoreType.DMA
-    return pl.pallas_call(
+    image, alpha, beta = pl.pallas_call(
         functools.partial(kernel, n_own, n_blk, low),
         out_shape=(out, out, out),
-        in_specs=[vmem] * 4,
+        in_specs=[pl.BlockSpec(memory_space=pl.ANY)] * 3,
         out_specs=(vmem,) * 3,
         scratch_shapes=[
+            pltpu.VMEM(points.shape, jnp.bfloat16),
+            pltpu.VMEM(direction.shape, jnp.float32),
+            pltpu.VMEM(direction.shape, jnp.float32),
+            dma((3,)),
             pltpu.VMEM((dim, n_row * width), jnp.bfloat16),
             pltpu.VMEM((n_col, dim + padded, width), jnp.bfloat16),
             pltpu.VMEM((1, n_row * width), jnp.float32),
             pltpu.VMEM((padded, n_row * width), jnp.float32),
             pltpu.VMEM((n_row, padded, width), jnp.bfloat16),
             pltpu.VMEM((n_row, padded, width), jnp.bfloat16),
-            pltpu.VMEM((n_own * n_blk, 4, width), jnp.float32),
+            pltpu.VMEM((n_own * n_blk, 1 if 3 * rhs <= width else 3, width), jnp.float32),
+            pltpu.VMEM((n_own * n_blk, 1, width), jnp.float32),
             dma((n_row,)), dma((n_row,)), dma((n_col,)), dma((n_col,)),
-            dma((n_row,)), dma((n_row,)), dma, dma,
+            dma((n_row,)), dma((n_row,)), dma((2,)), dma((2,)),
         ],
         compiler_params=pltpu.CompilerParams(collective_id=0, has_side_effects=True),
-    )(points, solution_field, residual, direction)
+    )(points, residual, direction)
+    return pl.pallas_call(
+        update, out_shape=(out, out, out), in_specs=[vmem] * 6, out_specs=(vmem,) * 3,
+    )(image, alpha, beta, solution_field, residual, direction)
 
 
 def solution(mesh):

time: 25.7 us -> 23.1 us (0.90)
  local copies, waits for them, and re-layouts: 2.69 us -> 0 us
    unnamed x7 -> x0, local copies, waits for them, and re-layouts: 2.69 us -> none
    pallas_call x0 -> x1, Pallas kernels: none -> 1.44 us  [local(): pl.pallas_call(update, out_shape=(out, out, out), in_specs=[vmem] * 6, ou...]
    pallas_call x1, Pallas kernels: 22.1 us -> 20.8 us  [local(): pl.pallas_call(functools.partial(kernel, n_own, n_blk, low), out_shape=(o...]
where the time goes in v2:
time: 23.1 us; the launch traced here: 22.9 us
  Pallas kernels  22.2 us (96%)
  between operations  0.64 us (3%)
    pallas_call x1, Pallas kernels, local(): pl.pallas_call(functools.partial(kernel, n_own, n_blk, low), out_shape=(o...  20.8 us
    pallas_call x1, Pallas kernels, local(): pl.pallas_call(update, out_shape=(out, out, out), in_specs=[vmem] * 6, ou...  1.44 us

profile of v2, /device:TPU:0, one launch (start us, length us, event | category | flops | bytes accessed | tf_op | source)
XLA Modules:
  0.0 22.9 jit_solution(8000912580203993127)
XLA Ops:
  0.6 20.8 %shard_map.67 = (f32[33,128]{1,0:T(8,128)}, f32[33,128]{1,0:T(8,128)}, f32[33,128]{1,0:T(8,128)}) custom-call(bf16[64,128]{1,0:T(8,128)(2,1)} %points_hbm.1, f32[33,128]{1,0:T(8,128)} %residual.1, f32[33,128]{1,0:T(8,128)} %direction.1), custom_call_target="tpu_custom_call" | custom-call | tf_op jit(solution)/shard_map/pallas_call | solution.py:224
  21.4 1.4 %shard_map.68 = (f32[33,128]{1,0:T(8,128)}, f32[33,128]{1,0:T(8,128)}, f32[33,128]{1,0:T(8,128)}) custom-call(f32[33,128]{1,0:T(8,128)} %get-tuple-element.6.image, f32[33,128]{1,0:T(8,128)} %get-tuple-element.7.alpha, f32[33,128]{1,0:T(8,128)} %get-tuple-element.8.beta, f32[33,128]{1,0:T(8,128)} %solution_field.1, f32[33,128]{1,0:T(8,128)} %residual.1, ...), custom_call_target="tpu_custom_call" | custom-call | tf_op jit(solution)/shard_map/pallas_call | solution.py:247

commit v3 on v2

--- a/solution.py
+++ b/solution.py
@@ -142,7 +142,7 @@
 
     for copy in row_copies:
         copy.wait_recv()
-    chunk = math.gcd(n_row * width, 2 * width)
+    chunk = math.gcd(n_row * width, 8 * width)
     n_chunk = n_row * width // chunk
     for c in range(n_chunk):
         wide = rows_ref[:, c * chunk:(c + 1) * chunk].astype(jnp.float32)
@@ -223,7 +223,7 @@
     dma = pltpu.SemaphoreType.DMA
     image, alpha, beta = pl.pallas_call(
         functools.partial(kernel, n_own, n_blk, low),
-        out_shape=(out, out, out),
+        out_shape=(pltpu.VMEM(direction.shape, jnp.float32),) * 3,
         in_specs=[pl.BlockSpec(memory_space=pl.ANY)] * 3,
         out_specs=(vmem,) * 3,
         scratch_shapes=[
@@ -244,9 +244,8 @@
         ],
         compiler_params=pltpu.CompilerParams(collective_id=0, has_side_effects=True),
     )(points, residual, direction)
-    return pl.pallas_call(
-        update, out_shape=(out, out, out), in_specs=[vmem] * 6, out_specs=(vmem,) * 3,
-    )(image, alpha, beta, solution_field, residual, direction)
+    residual_next = residual - alpha * image
+    return solution_field + alpha * direction, residual_next, residual_next + beta * direction
 
 
 def solution(mesh):

time: 23.1 us -> 20.3 us (0.88)
  Pallas kernels: 22.2 us -> 18.8 us
  other arithmetic: 0 us -> 0.63 us
    pallas_call x2 -> x1, Pallas kernels: 22.2 us -> 18.8 us  [local(): pl.pallas_call(functools.partial(kernel, n_own, n_blk, low), out_shape=(p...]
    add x0 -> x1, other arithmetic: none -> 0.63 us  [local(): residual_next + beta * direction]
where the time goes in v3:
time: 20.3 us; the launch traced here: 20.1 us
  Pallas kernels  18.8 us (93%)
  between operations  0.69 us (3%)
  other arithmetic  0.63 us (3%)
    pallas_call x1, Pallas kernels, local(): pl.pallas_call(functools.partial(kernel, n_own, n_blk, low), out_shape=(p...  18.8 us
    add x1, other arithmetic, local(): residual_next + beta * direction  0.63 us

profile of v3, /device:TPU:0, one launch (start us, length us, event | category | flops | bytes accessed | tf_op | source)
XLA Modules:
  0.0 20.1 jit_solution(2520459589847544347)
XLA Ops:
  0.6 0.0 copy-start.1
  0.6 0.0 copy-start
  0.7 0.0 copy-start.2
  0.7 18.8 %shard_map.67 = (f32[33,128]{1,0:T(8,128)S(1)}, f32[33,128]{1,0:T(8,128)S(1)}, f32[33,128]{1,0:T(8,128)S(1)}) custom-call(bf16[64,128]{1,0:T(8,128)(2,1)} %points_hbm.1, f32[33,128]{1,0:T(8,128)} %residual_hbm.1, f32[33,128]{1,0:T(8,128)} %direction_hbm.1), custom_call_target="tpu_custom_call" | custom-call | tf_op jit(solution)/shard_map/pallas_call | solution.py:224
  19.4 0.0 copy-done.1
  19.4 0.0 copy-done
  19.4 0.0 copy-done.2
  19.4 0.6 %multiply_add_fusion = (f32[33,128]{1,0:T(8,128)}, f32[33,128]{1,0:T(8,128)}, f32[33,128]{1,0:T(8,128)}) fusion(f32[33,128]{1,0:T(8,128)S(1)} %get-tuple-element.8, f32[33,128]{1,0:T(8,128)S(1)} %copy-done.1, f32[33,128]{1,0:T(8,128)S(1)} %copy-done, f32[33,128]{1,0:T(8,128)S(1)} %get-tuple-element.6, f32[33,128]{1,0:T(8,128)S(1)} %get-tuple-element.7, ...), kind=kLoop, calls=%fused_computation | loop fusion | flops 25344 | bytes 152064 | tf_op jit(solution)/shard_map/add | solution.py:248
Async XLA Ops:
  0.6 18.8 %copy-start.1 = (f32[33,128]{1,0:T(8,128)S(1)}, f32[33,128]{1,0:T(8,128)}, u32[]{:S(2)}) copy-start(f32[33,128]{1,0:T(8,128)} %direction_hbm.1) | copy-start | bytes 50692
  0.6 18.8 %copy-start = (f32[33,128]{1,0:T(8,128)S(1)}, f32[33,128]{1,0:T(8,128)}, u32[]{:S(2)}) copy-start(f32[33,128]{1,0:T(8,128)} %residual_hbm.1) | copy-start | bytes 50692
  0.7 18.8 %copy-start.2 = (f32[33,128]{1,0:T(8,128)S(1)}, f32[33,128]{1,0:T(8,128)}, u32[]{:S(2)}) copy-start(f32[33,128]{1,0:T(8,128)} %param.5) | copy-start | bytes 50692

commit v4 on v3

--- a/solution.py
+++ b/solution.py
@@ -28,7 +28,7 @@
 
 
 def kernel(n_own, n_blk, low, points_hbm, residual_hbm, direction_hbm, image_out, alpha_out, beta_out,
-           points_ref, residual_ref, direction_ref, load_sem, rows_ref, cols_ref, norms_ref, acc_ref, part_ref, back_ref, sums_ref, square_ref,
+           points_ref, residual_ref, direction_ref, load_sem, rows_ref, cols_ref, norms_ref, acc_ref, part_ref, back_ref, sums_ref,
            row_send, row_recv, col_send, col_recv, part_send, part_recv, sum_send, sum_recv):
     high = n_own // low
     n_row, n_col = low * n_blk, high
@@ -68,7 +68,7 @@
     for k in range(1, n_row):
         pl.semaphore_signal(barrier, inc=1, device_id=row_peer(k), device_id_type=MESH)
 
-    for load in loads:
+    for load in loads[:2]:
         load.wait()
     cols_ref[0, :dim, :] = points_ref[...]
     cols_ref[0, dim:, :] = jnp.zeros(cols_ref.shape[1:], jnp.bfloat16)[dim:]
@@ -100,8 +100,8 @@
     n_all = n_own * n_blk
 
     def place(i, count):
-        packed = count * rhs <= width
-        return (0, i * rhs) if packed else (i, 0)
+        per_line = max(1, width // rhs)
+        return (i // per_line, i % per_line * rhs)
 
     def to_sums(products, ref):
         for line in range(ref.shape[1]):
@@ -136,9 +136,9 @@
 
         return finish
 
+    loads[2].wait()
     residual = residual_ref[...]
     direction = direction_ref[...]
-    to_sums([residual * residual], square_ref)
 
     for copy in row_copies:
         copy.wait_recv()
@@ -183,22 +183,19 @@
                 copy.start()
                 part_copies.append(copy)
 
-    early = exchange(square_ref, sum_send.at[1], sum_recv.at[1])
     image = acc_ref[:, :width]
     for k in range(1, n_row):
         wait_bytes(back_ref.at[k], part_recv.at[k])
         image += back_ref[k].astype(jnp.float32)
     image = image[:rhs] + noise_level * direction
 
-    to_sums([direction * image, residual * image, image * image], sums_ref)
+    to_sums([residual * residual, direction * image, residual * image, image * image], sums_ref)
     late = exchange(sums_ref, sum_send.at[0], sum_recv.at[0])
     image_out[...] = image
     for copy in col_copies + row_copies + part_copies:
         copy.wait_send()
-    early()
     late()
-    rr = unpack(square_ref, 0, 1)
-    pq, rq, qq = (unpack(sums_ref, i, 3) for i in range(3))
+    rr, pq, rq, qq = (unpack(sums_ref, i, 4) for i in range(4))
     alpha = rr / pq
     new_sum = rr - 2.0 * alpha * rq + alpha * alpha * qq
     alpha_out[...] = jnp.broadcast_to(alpha, (rhs, width))
@@ -217,7 +214,7 @@
     n_row, n_col = low * n_blk, n_own // low
     dim, width = points.shape
     rhs = direction.shape[0]
-    padded = -(-rhs // 16) * 16
+    padded = -(-rhs // 8) * 8
     vmem = pl.BlockSpec(memory_space=pltpu.VMEM)
     out = jax.ShapeDtypeStruct(direction.shape, jnp.float32)
     dma = pltpu.SemaphoreType.DMA
@@ -237,10 +234,9 @@
             pltpu.VMEM((padded, n_row * width), jnp.float32),
             pltpu.VMEM((n_row, padded, width), jnp.bfloat16),
             pltpu.VMEM((n_row, padded, width), jnp.bfloat16),
-            pltpu.VMEM((n_own * n_blk, 1 if 3 * rhs <= width else 3, width), jnp.float32),
-            pltpu.VMEM((n_own * n_blk, 1, width), jnp.float32),
+            pltpu.VMEM((n_own * n_blk, -(-4 // max(1, width // rhs)), width), jnp.float32),
             dma((n_row,)), dma((n_row,)), dma((n_col,)), dma((n_col,)),
-            dma((n_row,)), dma((n_row,)), dma((2,)), dma((2,)),
+            dma((n_row,)), dma((n_row,)), dma((1,)), dma((1,)),
         ],
         compiler_params=pltpu.CompilerParams(collective_id=0, has_side_effects=True),
     )(points, residual, direction)

time: 20.3 us -> 20.1 us (level)
  no operation moved by 1% of the time
where the time goes in v4:
time: 20.1 us; the launch traced here: 20 us
  Pallas kernels  18.6 us (93%)
  between operations  0.69 us (3%)
  other arithmetic  0.63 us (3%)
    pallas_call x1, Pallas kernels, local(): pl.pallas_call(functools.partial(kernel, n_own, n_blk, low), out_shape=(p...  18.6 us
    add x1, other arithmetic, local(): residual_next + beta * direction  0.63 us

profile of v4, /device:TPU:0, one launch (start us, length us, event | category | flops | bytes accessed | tf_op | source)
XLA Modules:
  0.0 20.0 jit_solution(9707782825600825836)
XLA Ops:
  0.6 0.0 copy-start.1
  0.6 0.0 copy-start
  0.7 0.0 copy-start.2
  0.7 18.6 %shard_map.67 = (f32[33,128]{1,0:T(8,128)S(1)}, f32[33,128]{1,0:T(8,128)S(1)}, f32[33,128]{1,0:T(8,128)S(1)}) custom-call(bf16[64,128]{1,0:T(8,128)(2,1)} %points_hbm.1, f32[33,128]{1,0:T(8,128)} %residual_hbm.1, f32[33,128]{1,0:T(8,128)} %direction_hbm.1), custom_call_target="tpu_custom_call" | custom-call | tf_op jit(solution)/shard_map/pallas_call | solution.py:221
  19.3 0.0 copy-done.1
  19.3 0.0 copy-done
  19.3 0.0 copy-done.2
  19.3 0.6 %multiply_add_fusion = (f32[33,128]{1,0:T(8,128)}, f32[33,128]{1,0:T(8,128)}, f32[33,128]{1,0:T(8,128)}) fusion(f32[33,128]{1,0:T(8,128)S(1)} %get-tuple-element.8, f32[33,128]{1,0:T(8,128)S(1)} %copy-done.1, f32[33,128]{1,0:T(8,128)S(1)} %copy-done, f32[33,128]{1,0:T(8,128)S(1)} %get-tuple-element.6, f32[33,128]{1,0:T(8,128)S(1)} %get-tuple-element.7, ...), kind=kLoop, calls=%fused_computation | loop fusion | flops 25344 | bytes 152064 | tf_op jit(solution)/shard_map/add | solution.py:244
Async XLA Ops:
  0.6 18.7 %copy-start.1 = (f32[33,128]{1,0:T(8,128)S(1)}, f32[33,128]{1,0:T(8,128)}, u32[]{:S(2)}) copy-start(f32[33,128]{1,0:T(8,128)} %direction_hbm.1) | copy-start | bytes 50692
  0.6 18.7 %copy-start = (f32[33,128]{1,0:T(8,128)S(1)}, f32[33,128]{1,0:T(8,128)}, u32[]{:S(2)}) copy-start(f32[33,128]{1,0:T(8,128)} %residual_hbm.1) | copy-start | bytes 50692
  0.7 18.7 %copy-start.2 = (f32[33,128]{1,0:T(8,128)S(1)}, f32[33,128]{1,0:T(8,128)}, u32[]{:S(2)}) copy-start(f32[33,128]{1,0:T(8,128)} %param.5) | copy-start | bytes 50692
